TPU v7x, 32 devices: a whole 2x2x4 slice. The times are simulated.
32 devices in a mesh: groups: 2 (over x), seq: 16 (over z, y, core).
Axes of the slice: x: 2, y: 2, z: 4, core: 2. Of those that a mesh axis runs over, the one named last changes fastest.
Arguments:
- queries: bfloat16 [2048, 4096], P(('groups', 'seq')), parts along dimension 0, may hold values from -8 to 8
- keys: bfloat16 [2048, 512], P(('groups', 'seq')), parts along dimension 0, may hold values from -8 to 8
- values: bfloat16 [2048, 512], P(('groups', 'seq')), parts along dimension 0, may hold values from -6 to 6
- block_pairs: int32 [32], P('groups'), parts along dimension 0, may hold values from 0 to 15, each once
- decode_slots: int32 [32], P('groups'), parts along dimension 0, may hold values from 0 to 15, each once
Outputs:
- attended: bfloat16 [2048, 4096], P(('groups', 'seq')), parts along dimension 0
- decode_cache: bfloat16 [32, 256, 2, 128], P(('groups', 'seq')), parts along dimension 0
There are 2 independent parts, one for each index of `groups`. A program takes and returns all parts, laid end to end along the dimension named above; each array names one. Nothing has to cross between parts.
Inputs may be any that keep to these rules, and one draw needn't show every extreme that they name: `block_pairs`: each of 0 to 15 once. `decode_slots`: each of 0 to 15 once.
All inputs are finite; a program needn't handle non-finite values.
Results may differ from a plain program's by a relative error of at most 0.012.
The roundings to bfloat16 on the way count: a program that leaves them out, or rounds other values in their place, can miss the bound.
Values may be sent and summed in bfloat16 or wider, within the bound.
No kernel may reach another device: no remote copies, remote signals or barrier semaphores. Data moves between devices by JAX's collectives and lax.ppermute only.
A program may use at most 128 MiB of HBM per device.

v0:
```python
import functools
import math

import jax
import jax.numpy as jnp
from jax import lax
from jax.experimental import pallas as pl
from jax.experimental.pallas import tpu as pltpu
from jax.sharding import PartitionSpec as P


HD = 128
KVH = 4
GQ = 8
QH = 32

ROPE_BASE = 500000.0
NEGATIVE = -1e30
LOG2E = math.log2(math.e)

VMEM_SPEC = pl.BlockSpec(memory_space=pltpu.VMEM)
HBM_SPEC = pl.BlockSpec(memory_space=pltpu.HBM)
F32 = jnp.float32
BF16 = jnp.bfloat16


def params(mib):
    return pltpu.CompilerParams(vmem_limit_bytes=mib << 20)


def rotation_tables(block, devices, tok_dev):
    half_tok = tok_dev // 2
    row = lax.broadcasted_iota(jnp.int32, (tok_dev, HD), 0)
    lane = lax.broadcasted_iota(jnp.int32, (tok_dev, HD), 1)
    early = row < half_tok
    position = jnp.where(
        early, block * half_tok + row, (2 * devices - 1 - block) * half_tok + row - half_tok
    )
    low = lane < HD // 2
    index = jnp.where(low, lane, lane - HD // 2).astype(F32)
    frequency = jnp.exp(index * (-2.0 * math.log(ROPE_BASE) / HD))
    angle = position.astype(F32) * frequency
    sine = jnp.sin(angle)
    return jnp.cos(angle), jnp.where(low, -sine, sine)


def turn(block, cosine, sine):
    wide = block.astype(F32)
    return (wide * cosine + pltpu.roll(wide, HD // 2, 1) * sine).astype(BF16)


def prep_kernel(devices, pairs_hbm, k_hbm, v_hbm, kv_ref, trig_ref, pairs_ref, k_ref, sems):
    tok_dev = k_ref.shape[0]
    width = KVH * HD
    copies = [
        pltpu.make_async_copy(pairs_hbm, pairs_ref, sems.at[0]),
        pltpu.make_async_copy(k_hbm, k_ref, sems.at[1]),
        pltpu.make_async_copy(v_hbm, kv_ref.at[:, width:], sems.at[2]),
    ]
    for copy in copies:
        copy.start()
    copies[0].wait()
    cosine, sine = rotation_tables(pairs_ref[lax.axis_index("seq")], devices, tok_dev)
    trig_ref[:, :HD] = cosine
    trig_ref[:, HD:] = sine
    copies[1].wait()
    for g in range(KVH):
        cols = slice(g * HD, (g + 1) * HD)
        kv_ref[:, cols] = turn(k_ref[:, cols], cosine, sine)
    copies[2].wait()


def prep(pairs, keys, values):
    devices = lax.axis_size("seq")
    tok_dev = keys.shape[0]
    return pl.pallas_call(
        functools.partial(prep_kernel, devices),
        out_shape=(
            jax.ShapeDtypeStruct((tok_dev, 2 * KVH * HD), BF16),
            jax.ShapeDtypeStruct((tok_dev, 2 * HD), F32),
        ),
        in_specs=[HBM_SPEC] * 3,
        out_specs=(VMEM_SPEC,) * 2,
        scratch_shapes=[
            pltpu.SMEM(pairs.shape, jnp.int32),
            pltpu.VMEM(keys.shape, BF16),
            pltpu.SemaphoreType.DMA((3,)),
        ],
        compiler_params=params(8),
        name="prep",
    )(pairs, keys, values)


def turn_kernel(
    devices, q_hbm, pairs_hbm, slots_hbm, trig_ref, turned_ref, info_ref, q_ref, pairs_ref, slots_ref, sems
):
    tok_dev = q_ref.shape[0]
    half_tok = tok_dev // 2
    stride = devices // KVH
    width = GQ * HD
    copies = []
    for g in range(KVH):
        cols = pl.ds(g * width, width)
        copies.append(pltpu.make_async_copy(q_hbm.at[:, cols], q_ref.at[:, cols], sems.at[g]))
    copies.append(pltpu.make_async_copy(pairs_hbm, pairs_ref, sems.at[KVH]))
    copies.append(pltpu.make_async_copy(slots_hbm, slots_ref, sems.at[KVH + 1]))
    for copy in copies:
        copy.start()
    cosine, sine = trig_ref[:, :HD], trig_ref[:, HD:]
    for g in range(KVH):
        copies[g].wait()
        turned = [
            turn(q_ref[:, head * HD : (head + 1) * HD], cosine, sine)
            for head in range(g * GQ, (g + 1) * GQ)
        ]
        for half in range(2):
            part = [t[half * half_tok : (half + 1) * half_tok] for t in turned]
            turned_ref[half, g] = jnp.concatenate(part, axis=0).T
    copies[KVH].wait()
    copies[KVH + 1].wait()
    me = lax.axis_index("seq")
    lane = lax.broadcasted_iota(jnp.int32, (1, devices), 1)
    peers = jnp.zeros((1, devices), jnp.int32)
    for i in range(devices):
        peers = jnp.where(lane == i, pairs_ref[lax.bitwise_xor(me, i)], peers)
    slot = slots_ref[me]
    info_ref[0:1, :] = peers
    info_ref[1:2, :] = jnp.where(lane == 0, slot // stride, slot % stride)


def turn_queries(queries, pairs, slots, trig):
    devices = lax.axis_size("seq")
    rows = GQ * queries.shape[0] // 2
    return pl.pallas_call(
        functools.partial(turn_kernel, devices),
        out_shape=(
            jax.ShapeDtypeStruct((2, KVH, HD, rows), BF16),
            jax.ShapeDtypeStruct((2, devices), jnp.int32),
        ),
        in_specs=[HBM_SPEC] * 3 + [VMEM_SPEC],
        out_specs=(VMEM_SPEC,) * 2,
        scratch_shapes=[
            pltpu.VMEM(queries.shape, BF16),
            pltpu.SMEM(pairs.shape, jnp.int32),
            pltpu.SMEM(slots.shape, jnp.int32),
            pltpu.SemaphoreType.DMA((KVH + 2,)),
        ],
        compiler_params=params(8),
        name="turn",
    )(queries, pairs, slots, trig)


def fold(x):
    return x.reshape(x.shape[0] // 8, 8, x.shape[1])


def spread_max(x):
    for shift in (4, 2, 1):
        x = jnp.maximum(x, pltpu.roll(x, shift, 0))
    return x


def chunk_kernel(devices, offsets, counts, first, last, *refs):
    refs = list(refs)
    info_ref, turned_ref = refs.pop(0), refs.pop(0)
    block_refs = [refs.pop(0) for _ in counts]
    if not first:
        old_refs = [refs.pop(0) for _ in range(3)]
        old_cache_ref = refs.pop(0)
    if last:
        out_hbm, cache_hbm, out_ref, cache_ref, sems = refs
    else:
        new_refs = [refs.pop(0) for _ in range(3)]
        cache_ref = refs.pop(0)

    own = info_ref[0, 0]
    head, phase = info_ref[1, 0], info_ref[1, 1]
    tok_dev = block_refs[0].shape[-2]
    half_tok = tok_dev // 2
    stride = devices // KVH
    rows = GQ * half_tok

    where = []
    for ref, count in zip(block_refs, counts):
        where += [ref.at[i] for i in range(count)] if count else [ref]
    pair_of = [info_ref[0, offset] for offset in offsets]

    def gathered(col, half):
        return jnp.concatenate(
            [w[half * half_tok : (half + 1) * half_tok, pl.ds(col, HD)] for w in where], axis=0
        )

    per_block = half_tok // stride
    peers = len(where)
    out_rows = 2 * per_block * peers
    row = lax.broadcasted_iota(jnp.int32, (out_rows, peers * half_tok), 0)
    lane = lax.broadcasted_iota(jnp.int32, (out_rows, peers * half_tok), 1)
    source = (row // (2 * per_block)) * half_tok + (row % (2 * per_block)) // 2 * stride + phase
    hit = source == lane
    pick_key = jnp.where(hit & (row % 2 == 0), 1.0, 0.0).astype(BF16)
    pick_value = jnp.where(hit & (row % 2 == 1), 1.0, 0.0).astype(BF16)
    key_col = pl.multiple_of(head * HD, HD)
    value_col = pl.multiple_of((KVH + head) * HD, HD)
    if not first:
        cache_ref[...] = old_cache_ref[...]
    for half in range(2):
        picked = jnp.dot(pick_key, gathered(key_col, half), preferred_element_type=F32)
        picked += jnp.dot(pick_value, gathered(value_col, half), preferred_element_type=F32)
        picked = picked.astype(BF16)
        for i, pair in enumerate(pair_of):
            block = pair if half == 0 else 2 * devices - 1 - pair
            cache_ref[block] = picked[i * 2 * per_block : (i + 1) * 2 * per_block]
    copies = []
    if last:
        copies.append(pltpu.make_async_copy(cache_ref, cache_hbm, sems.at[KVH]))
        copies[0].start()

    scale = LOG2E / math.sqrt(HD)
    keys_half = len(where) * half_tok

    row = lax.broadcasted_iota(jnp.int32, (half_tok, HD), 0)
    lane = lax.broadcasted_iota(jnp.int32, (half_tok, HD), 1)

    def key_flags(distance):
        column = jnp.where(distance == 0, row, jnp.where(distance < 0, half_tok, HD))
        return jnp.where(lane == column, 1.0, 0.0).astype(BF16)

    early_flags = jnp.concatenate([key_flags(own - pair) for pair in pair_of], axis=0)
    late_flags = jnp.concatenate([key_flags(pair - own) for pair in pair_of], axis=0)
    blank = jnp.zeros((keys_half, HD), BF16)
    order = lax.broadcasted_iota(jnp.int32, (HD, rows), 0)
    token = lax.broadcasted_iota(jnp.int32, (HD, rows), 1) % half_tok
    barred = jnp.where((order > token) & (order <= half_tok), NEGATIVE, 0.0).astype(BF16)
    ones = jnp.ones((16, 2 * keys_half), BF16)

    def scores_of(g):
        key_early, key_late = gathered(g * HD, 0), gathered(g * HD, 1)
        query_early = jnp.concatenate([turned_ref[0, g], barred], axis=0)
        query_late = jnp.concatenate([turned_ref[1, g], barred], axis=0)
        early = jnp.dot(
            jnp.concatenate([key_early, early_flags], axis=1),
            query_early,
            preferred_element_type=F32,
        )
        late_keys = jnp.concatenate([key_early, key_late], axis=0)
        flags = jnp.concatenate([blank, late_flags], axis=0)
        late = jnp.dot(
            jnp.concatenate([late_keys, flags], axis=1), query_late, preferred_element_type=F32
        )
        return early, late

    def update(half, g, scores, values):
        index = half * KVH + g
        scores = fold(scores)
        top = spread_max(jnp.max(scores, axis=0)) * scale
        if not first:
            old_max = old_refs[0][index]
            top = jnp.maximum(old_max, top)
            factor = jnp.exp2(old_max - top)
        weights = jnp.exp2(scores * scale - top[None]).astype(BF16).reshape(-1, rows)
        both = jnp.dot(values, weights, preferred_element_type=F32)
        mixture, sums = fold(both[:HD]), both[HD : HD + 8]
        if not first:
            sums = old_refs[1][index] * factor + sums
            mixture = fold(old_refs[2][half, g]) * factor[None] + mixture
        if last:
            result = (mixture * (1.0 / sums)[None]).reshape(HD, rows).astype(BF16).T
            for r in range(GQ):
                col = (g * GQ + r) * HD
                out_ref[half * half_tok : (half + 1) * half_tok, col : col + HD] = result[
                    r * half_tok : (r + 1) * half_tok
                ]
        else:
            new_refs[0][index] = top
            new_refs[1][index] = sums
            new_refs[2][half, g] = mixture.reshape(HD, rows)

    scores = [scores_of(g) for g in range(KVH)]
    values = []
    for g in range(KVH):
        value_rows = jnp.concatenate(
            [gathered((KVH + g) * HD, 0), gathered((KVH + g) * HD, 1)], axis=0
        )
        values.append(jnp.concatenate([value_rows.T, ones], axis=0))
    for g in range(KVH):
        update(0, g, scores[g][0], values[g][:, :keys_half])
        update(1, g, scores[g][1], values[g])
        if last:
            cols = pl.ds(g * GQ * HD, GQ * HD)
            copies.append(
                pltpu.make_async_copy(out_ref.at[:, cols], out_hbm.at[:, cols], sems.at[g])
            )
            copies[-1].start()
    for copy in copies:
        copy.wait()


def attend_chunk(info, turned, blocks, offsets, counts, state, last):
    devices = lax.axis_size("seq")
    tok_dev = blocks[0].shape[-2]
    stride = devices // KVH
    rows = GQ * tok_dev // 2
    first = state is None
    operands = [info, turned, *blocks, *(state or ())]
    cache = jax.ShapeDtypeStruct((2 * devices, tok_dev // stride, HD), BF16)
    aliases, scratch = {}, []
    if last:
        out = jax.ShapeDtypeStruct((tok_dev, QH * HD), BF16)
        outs = (out, cache)
        scratch = [
            pltpu.VMEM(out.shape, BF16),
            pltpu.VMEM(cache.shape, BF16),
            pltpu.SemaphoreType.DMA((KVH + 1,)),
        ]
    else:
        small = jax.ShapeDtypeStruct((2 * KVH, 8, rows), F32)
        outs = (small, small, jax.ShapeDtypeStruct((2, KVH, HD, rows), F32), cache)
        if not first:
            aliases = {2 + len(blocks) + i: i for i in range(4)}
    work = len(offsets) * (tok_dev // 2) * rows * KVH * HD
    return pl.pallas_call(
        functools.partial(chunk_kernel, devices, offsets, counts, first, last),
        out_shape=outs,
        in_specs=[VMEM_SPEC] * len(operands),
        out_specs=tuple([HBM_SPEC if last else VMEM_SPEC] * len(outs)),
        scratch_shapes=scratch,
        input_output_aliases=aliases,
        compiler_params=params(24),
        cost_estimate=pl.CostEstimate(flops=12 * work, bytes_accessed=1 << 20, transcendentals=0),
        name="attend",
    )(*operands)


def swap(x, offset):
    devices = lax.axis_size("seq")
    return lax.ppermute(x, "seq", [(s, s ^ offset) for s in range(devices)])


def ring_order(outer):
    direct = [0] + [(1 << k) - 1 for k in range(1, outer.bit_length())]
    return direct + [step for step in range(outer) if step not in direct]


def layout_of(devices):
    cores = 2
    chips = devices // cores
    outer = 1 << -(-(chips.bit_length() - 1) // 2)
    return outer, chips // outer, cores


def whole_step(queries, keys, values, block_pairs, decode_slots):
    devices = lax.axis_size("seq")
    tok_dev = queries.shape[0]
    stride = devices // KVH
    outer, inner, cores = layout_of(devices)

    def hbm(x):
        return pltpu.with_memory_space_constraint(x, pltpu.HBM)

    pairs, slots = hbm(block_pairs), hbm(decode_slots)
    kv, trig = prep(pairs, hbm(keys), hbm(values))
    turned, info = turn_queries(hbm(queries), pairs, slots, trig)
    plane = inner * cores
    far = {0: kv}
    order = ring_order(outer)
    for step in order[1:]:
        full = (1 << step.bit_length()) - 1
        source = 0 if step == full else full
        far[step] = swap(far[source], (step ^ source) * plane)
    state = None
    zeros = (0,) * inner
    for step in order:
        near = [far[step]]
        for y in range(1, inner):
            near.append(swap(far[step], y * cores))
        here = tuple(step * plane + y * cores for y in range(inner))
        there = tuple(i + 1 for i in here)
        if step == order[-1]:
            first, rest = swap(near[0], 1), swap(jnp.stack(near[1:]), 1)
            pieces = [
                (f"a{step}", [*near, first], here + there[:1], (*zeros, 0)),
                ("aend", [rest], there[1:], (inner - 1,)),
            ]
        else:
            pair = swap(jnp.stack(near), 1)
            pieces = [(f"a{step}", [*near, pair], here + there, (*zeros, inner))]
        for name, blocks, offsets, counts in pieces:
            state = attend_chunk(
                info, turned, blocks, offsets, counts, state, name == "aend"
            )
    attended, cache = state
    return attended, cache.reshape(1, tok_dev * devices // stride, 2, HD)


def solution(mesh):
    placed = (
        P(("groups", "seq"), None),
        P(("groups", "seq"), None),
        P(("groups", "seq"), None),
        P("groups"),
        P("groups"),
    )
    return jax.shard_map(
        whole_step,
        mesh=mesh,
        in_specs=placed,
        out_specs=(P(("groups", "seq"), None), P(("groups", "seq"), None, None, None)),
        check_vma=False,
    )
```

profile of v0, /device:TPU:0, one launch (start us, length us, event | category | flops | bytes accessed | tf_op | source)
XLA Modules:
  0.0 33.2 jit_solution(18121937465830735198)
XLA Ops:
  0.6 1.0 %prep.1 = (bf16[64,1024]{1,0:T(8,128)(2,1)S(1)}, f32[64,256]{1,0:T(8,128)S(1)}) custom-call(s32[16]{0:T(128)} %pairs_hbm.3, bf16[64,512]{1,0:T(8,128)(2,1)} %k_hbm.1, bf16[64,512]{1,0:T(8,128)(2,1)} %v_hbm.1), custom_call_target="tpu_custom_call" | custom-call | tf_op jit(solution)/shard_map/prep/pallas_call | solution.py:76
  1.6 3.1 %collective-permute-start.7 = (bf16[64,1024]{1,0:T(8,128)(2,1)S(1)}, bf16[64,1024]{1,0:T(8,128)(2,1)S(1)}, u32[]{:S(2)}, u32[]{:S(2)}) collective-permute-start(bf16[64,1024]{1,0:T(8,128)(2,1)S(1)} %get-tuple-element.27.refs_2_), channel_id=1, source_target_pairs={{0,4},{1,5},{2,6},{3,7},{4,0},{5,1},{6,2},{7,3},{8,12},{9,13},{10,... | collective-permute-start | bytes 393224 | tf_op jit(solution)/shard_map/ppermute | solution.py:336
  4.7 2.5 %collective-permute-start = (bf16[64,1024]{1,0:T(8,128)(2,1)S(1)}, bf16[64,1024]{1,0:T(8,128)(2,1)S(1)}, u32[]{:S(2)}, u32[]{:S(2)}) collective-permute-start(bf16[64,1024]{1,0:T(8,128)(2,1)S(1)} %get-tuple-element.27.refs_2_), channel_id=1, source_target_pairs={{0,12},{1,13},{2,14},{3,15},{4,8},{5,9},{6,10},{7,11},{8,4},{9,5},... | collective-permute-start | bytes 393224 | tf_op jit(solution)/shard_map/ppermute | solution.py:336
  7.2 1.5 %collective-permute-start.10 = (bf16[64,1024]{1,0:T(8,128)(2,1)S(1)}, bf16[64,1024]{1,0:T(8,128)(2,1)S(1)}, u32[]{:S(2)}, u32[]{:S(2)}) collective-permute-start(bf16[64,1024]{1,0:T(8,128)(2,1)S(1)} %get-tuple-element.27.refs_2_), channel_id=1, source_target_pairs={{0,2},{1,3},{2,0},{3,1},{4,6},{5,7},{6,4},{7,5},{8,10},{9,11},{10,... | collective-permute-start | bytes 393224 | tf_op jit(solution)/shard_map/ppermute | solution.py:336
  8.7 0.0 collective-permute-done.7.refs_2_
  8.7 1.2 %collective-permute-start.8 = (bf16[64,1024]{1,0:T(8,128)(2,1)S(1)}, bf16[64,1024]{1,0:T(8,128)(2,1)S(1)}, u32[]{:S(2)}, u32[]{:S(2)}) collective-permute-start(bf16[64,1024]{1,0:T(8,128)(2,1)S(1)} %collective-permute-done.7.refs_2_), channel_id=1, source_target_pairs={{0,2},{1,3},{2,0},{3,1},{4,6},{5,7},{6,4},{7,5},{8,10},{9,11},{10,... | collective-permute-start | bytes 393224 | tf_op jit(solution)/shard_map/ppermute | solution.py:336
  9.9 3.4 %collective-permute-done.refs_2_ = bf16[64,1024]{1,0:T(8,128)(2,1)S(1)} collective-permute-done((bf16[64,1024]{1,0:T(8,128)(2,1)S(1)}, bf16[64,1024]{1,0:T(8,128)(2,1)S(1)}, u32[]{:S(2)}, u32[]{:S(2)}) %collective-permute-start) | collective-permute-done | bytes 131104 | tf_op jit(solution)/shard_map/ppermute | solution.py:336
  13.3 1.5 %collective-permute-start.5 = (bf16[64,1024]{1,0:T(8,128)(2,1)S(1)}, bf16[64,1024]{1,0:T(8,128)(2,1)S(1)}, u32[]{:S(2)}, u32[]{:S(2)}) collective-permute-start(bf16[64,1024]{1,0:T(8,128)(2,1)S(1)} %collective-permute-done.refs_2_), channel_id=1, source_target_pairs={{0,2},{1,3},{2,0},{3,1},{4,6},{5,7},{6,4},{7,5},{8,10},{9,11},{10,... | collective-permute-start | bytes 393224 | tf_op jit(solution)/shard_map/ppermute | solution.py:336
  14.8 0.0 collective-permute-done.10.refs_3_
  14.9 0.1 collective-permute-start.11
  14.9 0.6 %collective-permute-start.1 = (bf16[64,1024]{1,0:T(8,128)(2,1)S(1)}, bf16[64,1024]{1,0:T(8,128)(2,1)S(1)}, u32[]{:S(2)}, u32[]{:S(2)}) collective-permute-start(bf16[64,1024]{1,0:T(8,128)(2,1)S(1)} %collective-permute-done.refs_2_), channel_id=1, source_target_pairs={{0,4},{1,5},{2,6},{3,7},{4,0},{5,1},{6,2},{7,3},{8,12},{9,13},{10,... | collective-permute-start | bytes 393224 | tf_op jit(solution)/shard_map/ppermute | solution.py:336
  15.6 0.0 collective-permute-done.8.refs_3_
  15.6 0.2 collective-permute-start.9
  15.8 2.4 %collective-permute-done.5.refs_3_ = bf16[64,1024]{1,0:T(8,128)(2,1)S(1)} collective-permute-done((bf16[64,1024]{1,0:T(8,128)(2,1)S(1)}, bf16[64,1024]{1,0:T(8,128)(2,1)S(1)}, u32[]{:S(2)}, u32[]{:S(2)}) %collective-permute-start.5) | collective-permute-done | bytes 131104 | tf_op jit(solution)/shard_map/ppermute | solution.py:336
  18.3 0.1 collective-permute-start.6
  18.4 2.5 %collective-permute-done.1.refs_2_ = bf16[64,1024]{1,0:T(8,128)(2,1)S(1)} collective-permute-done((bf16[64,1024]{1,0:T(8,128)(2,1)S(1)}, bf16[64,1024]{1,0:T(8,128)(2,1)S(1)}, u32[]{:S(2)}, u32[]{:S(2)}) %collective-permute-start.1) | collective-permute-done | bytes 131104 | tf_op jit(solution)/shard_map/ppermute | solution.py:336
  20.8 0.5 %collective-permute-start.2 = (bf16[64,1024]{1,0:T(8,128)(2,1)S(1)}, bf16[64,1024]{1,0:T(8,128)(2,1)S(1)}, u32[]{:S(2)}, u32[]{:S(2)}) collective-permute-start(bf16[64,1024]{1,0:T(8,128)(2,1)S(1)} %collective-permute-done.1.refs_2_), channel_id=1, source_target_pairs={{0,2},{1,3},{2,0},{3,1},{4,6},{5,7},{6,4},{7,5},{8,10},{9,11},{10,... | collective-permute-start | bytes 393224 | tf_op jit(solution)/shard_map/ppermute | solution.py:336
  21.4 0.0 collective-permute-start.4
  21.4 4.5 %collective-permute-done.2.refs_3_ = bf16[64,1024]{1,0:T(8,128)(2,1)S(1)} collective-permute-done((bf16[64,1024]{1,0:T(8,128)(2,1)S(1)}, bf16[64,1024]{1,0:T(8,128)(2,1)S(1)}, u32[]{:S(2)}, u32[]{:S(2)}) %collective-permute-start.2) | collective-permute-done | bytes 131104 | tf_op jit(solution)/shard_map/ppermute | solution.py:336
  25.8 0.0 collective-permute-start.3
  25.8 1.7 %turn.1 = (bf16[2,4,128,256]{3,2,1,0:T(8,128)(2,1)S(1)}, s32[2,16]{1,0:T(2,128)S(1)}) custom-call(bf16[64,4096]{1,0:T(8,128)(2,1)} %q_hbm.1, s32[16]{0:T(128)} %pairs_hbm.3, s32[16]{0:T(128)} %slots_hbm.1, f32[64,256]{1,0:T(8,128)S(1)} %get-tuple-element.24.trig_ref), custom_call_target="tpu_custom_call" | custom-call | tf_op jit(solution)/shard_map/turn/pallas_call | solution.py:134
  27.6 0.0 collective-permute-done.11.refs_4_
  27.6 0.9 %attend.5 = (f32[8,8,256]{2,1,0:T(8,128)S(1)}, f32[8,8,256]{2,1,0:T(8,128)S(1)}, f32[2,4,128,256]{3,2,1,0:T(8,128)S(1)}, bf16[32,16,128]{2,1,0:T(8,128)(2,1)S(1)}) custom-call(s32[2,16]{1,0:T(2,128)S(1)} %get-tuple-element.25.refs_0_, bf16[2,4,128,256]{3,2,1,0:T(8,128)(2,1)S(1)} %get-tuple-element.26.refs_1_, ...), custom_call_target="tpu_custom_call" | custom-call | flops 201326592 | bytes 1048576 | tf_op jit(solution)/shard_map/attend/pallas_call | solution.py:321
  28.5 0.0 collective-permute-done.9.refs_4_
  28.5 1.1 %attend.6 = (f32[8,8,256]{2,1,0:T(8,128)S(1)}, f32[8,8,256]{2,1,0:T(8,128)S(1)}, f32[2,4,128,256]{3,2,1,0:T(8,128)S(1)}, bf16[32,16,128]{2,1,0:T(8,128)(2,1)S(1)}) custom-call(s32[2,16]{1,0:T(2,128)S(1)} %get-tuple-element.25.refs_0_, ...), custom_call_target="tpu_custom_call", output_to_operand_aliasing={{0}: (5, {}), {1}: (6, {}), {2}: (7, {}), {3}: (8, {})} | custom-call | flops 201326592 | bytes 1048576 | tf_op jit(solution)/shard_map/attend/pallas_call | solution.py:321
  29.6 0.0 collective-permute-done.6.refs_4_
  29.6 1.1 %attend.7 = (f32[8,8,256]{2,1,0:T(8,128)S(1)}, f32[8,8,256]{2,1,0:T(8,128)S(1)}, f32[2,4,128,256]{3,2,1,0:T(8,128)S(1)}, bf16[32,16,128]{2,1,0:T(8,128)(2,1)S(1)}) custom-call(s32[2,16]{1,0:T(2,128)S(1)} %get-tuple-element.25.refs_0_, ...), custom_call_target="tpu_custom_call", output_to_operand_aliasing={{0}: (5, {}), {1}: (6, {}), {2}: (7, {}), {3}: (8, {})} | custom-call | flops 201326592 | bytes 1048576 | tf_op jit(solution)/shard_map/attend/pallas_call | solution.py:321
  30.7 0.0 collective-permute-done.4.refs_4_
  30.7 1.0 %attend.8 = (f32[8,8,256]{2,1,0:T(8,128)S(1)}, f32[8,8,256]{2,1,0:T(8,128)S(1)}, f32[2,4,128,256]{3,2,1,0:T(8,128)S(1)}, bf16[32,16,128]{2,1,0:T(8,128)(2,1)S(1)}) custom-call(s32[2,16]{1,0:T(2,128)S(1)} %get-tuple-element.25.refs_0_, ...), custom_call_target="tpu_custom_call", output_to_operand_aliasing={{0}: (5, {}), {1}: (6, {}), {2}: (7, {}), {3}: (8, {})} | custom-call | flops 150994944 | bytes 1048576 | tf_op jit(solution)/shard_map/attend/pallas_call | solution.py:321
  31.7 0.0 collective-permute-done.3.refs_2_
  31.7 1.4 %attend.9 = (bf16[64,4096]{1,0:T(8,128)(2,1)}, bf16[32,16,128]{2,1,0:T(8,128)(2,1)}) custom-call(s32[2,16]{1,0:T(2,128)S(1)} %get-tuple-element.25.refs_0_, bf16[2,4,128,256]{3,2,1,0:T(8,128)(2,1)S(1)} %get-tuple-element.26.refs_1_, bf16[1,64,1024]{2,1,0:T(8,128)(2,1)S(1)} %collective-permute-done.3.refs_2_, f32[8,8,256]{2,1,0:T(8,128)S(1)} %get-tuple-element.40.refs_3_, ...), custom_call_target="tpu_custom_call" | custom-call | flops 50331648 | bytes 1048576 | tf_op jit(solution)/shard_map/attend/pallas_call | solution.py:321
  (3 shorter events, 0.1 us)
Async XLA Ops:
  1.6 7.1 %collective-permute-start.7 = (bf16[64,1024]{1,0:T(8,128)(2,1)S(1)}, bf16[64,1024]{1,0:T(8,128)(2,1)S(1)}, u32[]{:S(2)}, u32[]{:S(2)}) collective-permute-start(bf16[64,1024]{1,0:T(8,128)(2,1)S(1)} %get-tuple-element.27.refs_2_), channel_id=1, source_target_pairs={{0,4},{1,5},{2,6},{3,7},{4,0},{5,1},{6,2},{7,3},{8,12},{9,13},{10,... | collective-permute-start | bytes 393224 | tf_op jit(solution)/shard_map/ppermute | solution.py:336
  4.7 8.6 %collective-permute-start = (bf16[64,1024]{1,0:T(8,128)(2,1)S(1)}, bf16[64,1024]{1,0:T(8,128)(2,1)S(1)}, u32[]{:S(2)}, u32[]{:S(2)}) collective-permute-start(bf16[64,1024]{1,0:T(8,128)(2,1)S(1)} %get-tuple-element.27.refs_2_), channel_id=1, source_target_pairs={{0,12},{1,13},{2,14},{3,15},{4,8},{5,9},{6,10},{7,11},{8,4},{9,5},... | collective-permute-start | bytes 393224 | tf_op jit(solution)/shard_map/ppermute | solution.py:336
  7.2 7.6 %collective-permute-start.10 = (bf16[64,1024]{1,0:T(8,128)(2,1)S(1)}, bf16[64,1024]{1,0:T(8,128)(2,1)S(1)}, u32[]{:S(2)}, u32[]{:S(2)}) collective-permute-start(bf16[64,1024]{1,0:T(8,128)(2,1)S(1)} %get-tuple-element.27.refs_2_), channel_id=1, source_target_pairs={{0,2},{1,3},{2,0},{3,1},{4,6},{5,7},{6,4},{7,5},{8,10},{9,11},{10,... | collective-permute-start | bytes 393224 | tf_op jit(solution)/shard_map/ppermute | solution.py:336
  8.7 6.9 %collective-permute-start.8 = (bf16[64,1024]{1,0:T(8,128)(2,1)S(1)}, bf16[64,1024]{1,0:T(8,128)(2,1)S(1)}, u32[]{:S(2)}, u32[]{:S(2)}) collective-permute-start(bf16[64,1024]{1,0:T(8,128)(2,1)S(1)} %collective-permute-done.7.refs_2_), channel_id=1, source_target_pairs={{0,2},{1,3},{2,0},{3,1},{4,6},{5,7},{6,4},{7,5},{8,10},{9,11},{10,... | collective-permute-start | bytes 393224 | tf_op jit(solution)/shard_map/ppermute | solution.py:336
  13.3 5.0 %collective-permute-start.5 = (bf16[64,1024]{1,0:T(8,128)(2,1)S(1)}, bf16[64,1024]{1,0:T(8,128)(2,1)S(1)}, u32[]{:S(2)}, u32[]{:S(2)}) collective-permute-start(bf16[64,1024]{1,0:T(8,128)(2,1)S(1)} %collective-permute-done.refs_2_), channel_id=1, source_target_pairs={{0,2},{1,3},{2,0},{3,1},{4,6},{5,7},{6,4},{7,5},{8,10},{9,11},{10,... | collective-permute-start | bytes 393224 | tf_op jit(solution)/shard_map/ppermute | solution.py:336
  14.9 12.7 %collective-permute-start.11 = (bf16[2,64,1024]{2,1,0:T(8,128)(2,1)S(1)}, bf16[2,64,1024]{2,1,0:T(8,128)(2,1)S(1)}, u32[]{:S(2)}, u32[]{:S(2)}) collective-permute-start(bf16[2,64,1024]{2,1,0:T(8,128)(2,1)S(1)} %pad_maximum_fusion.2), channel_id=1, source_target_pairs={{0,1},{1,0},{2,3},{3,2},{4,5},{5,4},{6,7},{7,6},{8,9},{9,8},{10,11... | collective-permute-start | bytes 786440 | tf_op jit(solution)/shard_map/ppermute | solution.py:336
  14.9 5.9 %collective-permute-start.1 = (bf16[64,1024]{1,0:T(8,128)(2,1)S(1)}, bf16[64,1024]{1,0:T(8,128)(2,1)S(1)}, u32[]{:S(2)}, u32[]{:S(2)}) collective-permute-start(bf16[64,1024]{1,0:T(8,128)(2,1)S(1)} %collective-permute-done.refs_2_), channel_id=1, source_target_pairs={{0,4},{1,5},{2,6},{3,7},{4,0},{5,1},{6,2},{7,3},{8,12},{9,13},{10,... | collective-permute-start | bytes 393224 | tf_op jit(solution)/shard_map/ppermute | solution.py:336
  15.6 12.8 %collective-permute-start.9 = (bf16[2,64,1024]{2,1,0:T(8,128)(2,1)S(1)}, bf16[2,64,1024]{2,1,0:T(8,128)(2,1)S(1)}, u32[]{:S(2)}, u32[]{:S(2)}) collective-permute-start(bf16[2,64,1024]{2,1,0:T(8,128)(2,1)S(1)} %pad_maximum_fusion.1), channel_id=1, source_target_pairs={{0,1},{1,0},{2,3},{3,2},{4,5},{5,4},{6,7},{7,6},{8,9},{9,8},{10,11... | collective-permute-start | bytes 786440 | tf_op jit(solution)/shard_map/ppermute | solution.py:336
  18.3 11.3 %collective-permute-start.6 = (bf16[2,64,1024]{2,1,0:T(8,128)(2,1)S(1)}, bf16[2,64,1024]{2,1,0:T(8,128)(2,1)S(1)}, u32[]{:S(2)}, u32[]{:S(2)}) collective-permute-start(bf16[2,64,1024]{2,1,0:T(8,128)(2,1)S(1)} %pad_maximum_fusion), channel_id=1, source_target_pairs={{0,1},{1,0},{2,3},{3,2},{4,5},{5,4},{6,7},{7,6},{8,9},{9,8},{10,11... | collective-permute-start | bytes 786440 | tf_op jit(solution)/shard_map/ppermute | solution.py:336
  20.8 5.0 %collective-permute-start.2 = (bf16[64,1024]{1,0:T(8,128)(2,1)S(1)}, bf16[64,1024]{1,0:T(8,128)(2,1)S(1)}, u32[]{:S(2)}, u32[]{:S(2)}) collective-permute-start(bf16[64,1024]{1,0:T(8,128)(2,1)S(1)} %collective-permute-done.1.refs_2_), channel_id=1, source_target_pairs={{0,2},{1,3},{2,0},{3,1},{4,6},{5,7},{6,4},{7,5},{8,10},{9,11},{10,... | collective-permute-start | bytes 393224 | tf_op jit(solution)/shard_map/ppermute | solution.py:336
  21.4 9.3 %collective-permute-start.4 = (bf16[64,1024]{1,0:T(8,128)(2,1)S(1)}, bf16[64,1024]{1,0:T(8,128)(2,1)S(1)}, u32[]{:S(2)}, u32[]{:S(2)}) collective-permute-start(bf16[64,1024]{1,0:T(8,128)(2,1)S(1)} %collective-permute-done.1.refs_2_), channel_id=1, source_target_pairs={{0,1},{1,0},{2,3},{3,2},{4,5},{5,4},{6,7},{7,6},{8,9},{9,8},{10,11... | collective-permute-start | bytes 393224 | tf_op jit(solution)/shard_map/ppermute | solution.py:336
  25.8 5.9 %collective-permute-start.3 = (bf16[1,64,1024]{2,1,0:T(8,128)(2,1)S(1)}, bf16[1,64,1024]{2,1,0:T(8,128)(2,1)S(1)}, u32[]{:S(2)}, u32[]{:S(2)}) collective-permute-start(bf16[1,64,1024]{2,1,0:T(8,128)(2,1)S(1)} %bitcast.14), channel_id=1, source_target_pairs={{0,1},{1,0},{2,3},{3,2},{4,5},{5,4},{6,7},{7,6},{8,9},{9,8},{10,11... | collective-permute-start | bytes 393224 | tf_op jit(solution)/shard_map/ppermute | solution.py:336
where the time goes:
time: 33.4 us; the launch traced here: 33.2 us
  waiting for transfers between devices  12.8 us (38%)
  starting transfers between devices  11.3 us (34%)
  Pallas kernels  8.22 us (25%)
  between operations  0.74 us (2%)
    ppermute x12, waiting for transfers between devices, swap(): return lax.ppermute(x, 'seq', [(s, s ^ offset) for s in range(devices)])  12.8 us
    ppermute x12, starting transfers between devices, swap(): return lax.ppermute(x, 'seq', [(s, s ^ offset) for s in range(devices)])  11.3 us
    pallas_call x5, Pallas kernels, attend_chunk(): pl.pallas_call(functools.partial(chunk_kernel, devices, offsets, counts,...  5.53 us
    pallas_call x1, Pallas kernels, turn_queries(): pl.pallas_call(functools.partial(turn_kernel, devices), out_shape=(jax.Sh...  1.72 us
    pallas_call x1, Pallas kernels, prep(): pl.pallas_call(functools.partial(prep_kernel, devices), out_shape=(jax.Sh...  0.96 us
  transfers between devices with their start and end apart: 12, of which 4 were waited for; matrix products, arithmetic and copies ran while one was open for 0% of the time, Pallas kernels for 18%

commit v1 on v0

--- a/solution.py
+++ b/solution.py
@@ -233,6 +233,25 @@
     barred = jnp.where((order > token) & (order <= half_tok), NEGATIVE, 0.0).astype(BF16)
     ones = jnp.ones((16, 2 * keys_half), BF16)
 
+    def masked_scores_of(g):
+        key_early, key_late = gathered(g * HD, 0), gathered(g * HD, 1)
+        ahead = lax.broadcasted_iota(jnp.int32, (half_tok, rows), 0) - (
+            lax.broadcasted_iota(jnp.int32, (half_tok, rows), 1) % half_tok
+        )
+        early_ok = jnp.concatenate([ahead <= half_tok * (own - pair) for pair in pair_of], axis=0)
+        late_ok = jnp.concatenate([ahead <= half_tok * (pair - own) for pair in pair_of], axis=0)
+        early = jnp.dot(key_early, turned_ref[0, g], preferred_element_type=F32)
+        late = jnp.dot(
+            jnp.concatenate([key_early, key_late], axis=0),
+            turned_ref[1, g],
+            preferred_element_type=F32,
+        )
+        late_half = jnp.where(late_ok, late[keys_half:], NEGATIVE)
+        return (
+            jnp.where(early_ok, early, NEGATIVE),
+            jnp.concatenate([late[:keys_half], late_half], axis=0),
+        )
+
     def scores_of(g):
         key_early, key_late = gathered(g * HD, 0), gathered(g * HD, 1)
         query_early = jnp.concatenate([turned_ref[0, g], barred], axis=0)
@@ -275,7 +294,8 @@
             new_refs[1][index] = sums
             new_refs[2][half, g] = mixture.reshape(HD, rows)
 
-    scores = [scores_of(g) for g in range(KVH)]
+    score = masked_scores_of if last else scores_of
+    scores = [score(g) for g in range(KVH)]
     values = []
     for g in range(KVH):
         value_rows = jnp.concatenate(

time: 33.4 us -> 33.3 us (level)
  no operation moved by 1% of the time
where the time goes in v1:
time: 33.3 us; the launch traced here: 33.1 us
  waiting for transfers between devices  12.8 us (38%)
  starting transfers between devices  11.3 us (34%)
  Pallas kernels  8.21 us (25%)
  between operations  0.74 us (2%)
    ppermute x12, waiting for transfers between devices, swap(): return lax.ppermute(x, 'seq', [(s, s ^ offset) for s in range(devices)])  12.8 us
    ppermute x12, starting transfers between devices, swap(): return lax.ppermute(x, 'seq', [(s, s ^ offset) for s in range(devices)])  11.3 us
    pallas_call x5, Pallas kernels, attend_chunk(): pl.pallas_call(functools.partial(chunk_kernel, devices, offsets, counts,...  5.52 us
    pallas_call x1, Pallas kernels, turn_queries(): pl.pallas_call(functools.partial(turn_kernel, devices), out_shape=(jax.Sh...  1.72 us
    pallas_call x1, Pallas kernels, prep(): pl.pallas_call(functools.partial(prep_kernel, devices), out_shape=(jax.Sh...  0.96 us
  transfers between devices with their start and end apart: 12, of which 4 were waited for; matrix products, arithmetic and copies ran while one was open for 0% of the time, Pallas kernels for 18%

profile of v1, /device:TPU:0, one launch (start us, length us, event | category | flops | bytes accessed | tf_op | source)
XLA Modules:
  0.0 33.1 jit_solution(499285547931816510)
XLA Ops:
  0.6 1.0 %prep.1 = (bf16[64,1024]{1,0:T(8,128)(2,1)S(1)}, f32[64,256]{1,0:T(8,128)S(1)}) custom-call(s32[16]{0:T(128)} %pairs_hbm.3, bf16[64,512]{1,0:T(8,128)(2,1)} %k_hbm.1, bf16[64,512]{1,0:T(8,128)(2,1)} %v_hbm.1), custom_call_target="tpu_custom_call" | custom-call | tf_op jit(solution)/shard_map/prep/pallas_call | solution.py:76
  1.6 3.1 %collective-permute-start.7 = (bf16[64,1024]{1,0:T(8,128)(2,1)S(1)}, bf16[64,1024]{1,0:T(8,128)(2,1)S(1)}, u32[]{:S(2)}, u32[]{:S(2)}) collective-permute-start(bf16[64,1024]{1,0:T(8,128)(2,1)S(1)} %get-tuple-element.27.refs_2_), channel_id=1, source_target_pairs={{0,4},{1,5},{2,6},{3,7},{4,0},{5,1},{6,2},{7,3},{8,12},{9,13},{10,... | collective-permute-start | bytes 393224 | tf_op jit(solution)/shard_map/ppermute | solution.py:356
  4.7 2.5 %collective-permute-start = (bf16[64,1024]{1,0:T(8,128)(2,1)S(1)}, bf16[64,1024]{1,0:T(8,128)(2,1)S(1)}, u32[]{:S(2)}, u32[]{:S(2)}) collective-permute-start(bf16[64,1024]{1,0:T(8,128)(2,1)S(1)} %get-tuple-element.27.refs_2_), channel_id=1, source_target_pairs={{0,12},{1,13},{2,14},{3,15},{4,8},{5,9},{6,10},{7,11},{8,4},{9,5},... | collective-permute-start | bytes 393224 | tf_op jit(solution)/shard_map/ppermute | solution.py:356
  7.2 1.5 %collective-permute-start.10 = (bf16[64,1024]{1,0:T(8,128)(2,1)S(1)}, bf16[64,1024]{1,0:T(8,128)(2,1)S(1)}, u32[]{:S(2)}, u32[]{:S(2)}) collective-permute-start(bf16[64,1024]{1,0:T(8,128)(2,1)S(1)} %get-tuple-element.27.refs_2_), channel_id=1, source_target_pairs={{0,2},{1,3},{2,0},{3,1},{4,6},{5,7},{6,4},{7,5},{8,10},{9,11},{10,... | collective-permute-start | bytes 393224 | tf_op jit(solution)/shard_map/ppermute | solution.py:356
  8.7 0.0 collective-permute-done.7.refs_2_
  8.7 1.2 %collective-permute-start.8 = (bf16[64,1024]{1,0:T(8,128)(2,1)S(1)}, bf16[64,1024]{1,0:T(8,128)(2,1)S(1)}, u32[]{:S(2)}, u32[]{:S(2)}) collective-permute-start(bf16[64,1024]{1,0:T(8,128)(2,1)S(1)} %collective-permute-done.7.refs_2_), channel_id=1, source_target_pairs={{0,2},{1,3},{2,0},{3,1},{4,6},{5,7},{6,4},{7,5},{8,10},{9,11},{10,... | collective-permute-start | bytes 393224 | tf_op jit(solution)/shard_map/ppermute | solution.py:356
  9.9 3.4 %collective-permute-done.refs_2_ = bf16[64,1024]{1,0:T(8,128)(2,1)S(1)} collective-permute-done((bf16[64,1024]{1,0:T(8,128)(2,1)S(1)}, bf16[64,1024]{1,0:T(8,128)(2,1)S(1)}, u32[]{:S(2)}, u32[]{:S(2)}) %collective-permute-start) | collective-permute-done | bytes 131104 | tf_op jit(solution)/shard_map/ppermute | solution.py:356
  13.3 1.5 %collective-permute-start.5 = (bf16[64,1024]{1,0:T(8,128)(2,1)S(1)}, bf16[64,1024]{1,0:T(8,128)(2,1)S(1)}, u32[]{:S(2)}, u32[]{:S(2)}) collective-permute-start(bf16[64,1024]{1,0:T(8,128)(2,1)S(1)} %collective-permute-done.refs_2_), channel_id=1, source_target_pairs={{0,2},{1,3},{2,0},{3,1},{4,6},{5,7},{6,4},{7,5},{8,10},{9,11},{10,... | collective-permute-start | bytes 393224 | tf_op jit(solution)/shard_map/ppermute | solution.py:356
  14.8 0.0 collective-permute-done.10.refs_3_
  14.9 0.1 collective-permute-start.11
  14.9 0.6 %collective-permute-start.1 = (bf16[64,1024]{1,0:T(8,128)(2,1)S(1)}, bf16[64,1024]{1,0:T(8,128)(2,1)S(1)}, u32[]{:S(2)}, u32[]{:S(2)}) collective-permute-start(bf16[64,1024]{1,0:T(8,128)(2,1)S(1)} %collective-permute-done.refs_2_), channel_id=1, source_target_pairs={{0,4},{1,5},{2,6},{3,7},{4,0},{5,1},{6,2},{7,3},{8,12},{9,13},{10,... | collective-permute-start | bytes 393224 | tf_op jit(solution)/shard_map/ppermute | solution.py:356
  15.6 0.0 collective-permute-done.8.refs_3_
  15.6 0.2 collective-permute-start.9
  15.8 2.4 %collective-permute-done.5.refs_3_ = bf16[64,1024]{1,0:T(8,128)(2,1)S(1)} collective-permute-done((bf16[64,1024]{1,0:T(8,128)(2,1)S(1)}, bf16[64,1024]{1,0:T(8,128)(2,1)S(1)}, u32[]{:S(2)}, u32[]{:S(2)}) %collective-permute-start.5) | collective-permute-done | bytes 131104 | tf_op jit(solution)/shard_map/ppermute | solution.py:356
  18.3 0.1 collective-permute-start.6
  18.4 2.5 %collective-permute-done.1.refs_2_ = bf16[64,1024]{1,0:T(8,128)(2,1)S(1)} collective-permute-done((bf16[64,1024]{1,0:T(8,128)(2,1)S(1)}, bf16[64,1024]{1,0:T(8,128)(2,1)S(1)}, u32[]{:S(2)}, u32[]{:S(2)}) %collective-permute-start.1) | collective-permute-done | bytes 131104 | tf_op jit(solution)/shard_map/ppermute | solution.py:356
  20.8 0.5 %collective-permute-start.2 = (bf16[64,1024]{1,0:T(8,128)(2,1)S(1)}, bf16[64,1024]{1,0:T(8,128)(2,1)S(1)}, u32[]{:S(2)}, u32[]{:S(2)}) collective-permute-start(bf16[64,1024]{1,0:T(8,128)(2,1)S(1)} %collective-permute-done.1.refs_2_), channel_id=1, source_target_pairs={{0,2},{1,3},{2,0},{3,1},{4,6},{5,7},{6,4},{7,5},{8,10},{9,11},{10,... | collective-permute-start | bytes 393224 | tf_op jit(solution)/shard_map/ppermute | solution.py:356
  21.4 0.0 collective-permute-start.4
  21.4 4.5 %collective-permute-done.2.refs_3_ = bf16[64,1024]{1,0:T(8,128)(2,1)S(1)} collective-permute-done((bf16[64,1024]{1,0:T(8,128)(2,1)S(1)}, bf16[64,1024]{1,0:T(8,128)(2,1)S(1)}, u32[]{:S(2)}, u32[]{:S(2)}) %collective-permute-start.2) | collective-permute-done | bytes 131104 | tf_op jit(solution)/shard_map/ppermute | solution.py:356
  25.8 0.0 collective-permute-start.3
  25.8 1.7 %turn.1 = (bf16[2,4,128,256]{3,2,1,0:T(8,128)(2,1)S(1)}, s32[2,16]{1,0:T(2,128)S(1)}) custom-call(bf16[64,4096]{1,0:T(8,128)(2,1)} %q_hbm.1, s32[16]{0:T(128)} %pairs_hbm.3, s32[16]{0:T(128)} %slots_hbm.1, f32[64,256]{1,0:T(8,128)S(1)} %get-tuple-element.24.trig_ref), custom_call_target="tpu_custom_call" | custom-call | tf_op jit(solution)/shard_map/turn/pallas_call | solution.py:134
  27.6 0.0 collective-permute-done.11.refs_4_
  27.6 0.9 %attend.5 = (f32[8,8,256]{2,1,0:T(8,128)S(1)}, f32[8,8,256]{2,1,0:T(8,128)S(1)}, f32[2,4,128,256]{3,2,1,0:T(8,128)S(1)}, bf16[32,16,128]{2,1,0:T(8,128)(2,1)S(1)}) custom-call(s32[2,16]{1,0:T(2,128)S(1)} %get-tuple-element.25.refs_0_, bf16[2,4,128,256]{3,2,1,0:T(8,128)(2,1)S(1)} %get-tuple-element.26.refs_1_, ...), custom_call_target="tpu_custom_call" | custom-call | flops 201326592 | bytes 1048576 | tf_op jit(solution)/shard_map/attend/pallas_call | solution.py:341
  28.5 0.0 collective-permute-done.9.refs_4_
  28.5 1.1 %attend.6 = (f32[8,8,256]{2,1,0:T(8,128)S(1)}, f32[8,8,256]{2,1,0:T(8,128)S(1)}, f32[2,4,128,256]{3,2,1,0:T(8,128)S(1)}, bf16[32,16,128]{2,1,0:T(8,128)(2,1)S(1)}) custom-call(s32[2,16]{1,0:T(2,128)S(1)} %get-tuple-element.25.refs_0_, ...), custom_call_target="tpu_custom_call", output_to_operand_aliasing={{0}: (5, {}), {1}: (6, {}), {2}: (7, {}), {3}: (8, {})} | custom-call | flops 201326592 | bytes 1048576 | tf_op jit(solution)/shard_map/attend/pallas_call | solution.py:341
  29.6 0.0 collective-permute-done.6.refs_4_
  29.6 1.1 %attend.7 = (f32[8,8,256]{2,1,0:T(8,128)S(1)}, f32[8,8,256]{2,1,0:T(8,128)S(1)}, f32[2,4,128,256]{3,2,1,0:T(8,128)S(1)}, bf16[32,16,128]{2,1,0:T(8,128)(2,1)S(1)}) custom-call(s32[2,16]{1,0:T(2,128)S(1)} %get-tuple-element.25.refs_0_, ...), custom_call_target="tpu_custom_call", output_to_operand_aliasing={{0}: (5, {}), {1}: (6, {}), {2}: (7, {}), {3}: (8, {})} | custom-call | flops 201326592 | bytes 1048576 | tf_op jit(solution)/shard_map/attend/pallas_call | solution.py:341
  30.7 0.0 collective-permute-done.4.refs_4_
  30.7 1.0 %attend.8 = (f32[8,8,256]{2,1,0:T(8,128)S(1)}, f32[8,8,256]{2,1,0:T(8,128)S(1)}, f32[2,4,128,256]{3,2,1,0:T(8,128)S(1)}, bf16[32,16,128]{2,1,0:T(8,128)(2,1)S(1)}) custom-call(s32[2,16]{1,0:T(2,128)S(1)} %get-tuple-element.25.refs_0_, ...), custom_call_target="tpu_custom_call", output_to_operand_aliasing={{0}: (5, {}), {1}: (6, {}), {2}: (7, {}), {3}: (8, {})} | custom-call | flops 150994944 | bytes 1048576 | tf_op jit(solution)/shard_map/attend/pallas_call | solution.py:341
  31.7 0.0 collective-permute-done.3.refs_2_
  31.7 1.4 %attend.9 = (bf16[64,4096]{1,0:T(8,128)(2,1)}, bf16[32,16,128]{2,1,0:T(8,128)(2,1)}) custom-call(s32[2,16]{1,0:T(2,128)S(1)} %get-tuple-element.25.refs_0_, bf16[2,4,128,256]{3,2,1,0:T(8,128)(2,1)S(1)} %get-tuple-element.26.refs_1_, bf16[1,64,1024]{2,1,0:T(8,128)(2,1)S(1)} %collective-permute-done.3.refs_2_, f32[8,8,256]{2,1,0:T(8,128)S(1)} %get-tuple-element.40.refs_3_, ...), custom_call_target="tpu_custom_call" | custom-call | flops 50331648 | bytes 1048576 | tf_op jit(solution)/shard_map/attend/pallas_call | solution.py:341
  (3 shorter events, 0.1 us)
Async XLA Ops:
  1.6 7.1 %collective-permute-start.7 = (bf16[64,1024]{1,0:T(8,128)(2,1)S(1)}, bf16[64,1024]{1,0:T(8,128)(2,1)S(1)}, u32[]{:S(2)}, u32[]{:S(2)}) collective-permute-start(bf16[64,1024]{1,0:T(8,128)(2,1)S(1)} %get-tuple-element.27.refs_2_), channel_id=1, source_target_pairs={{0,4},{1,5},{2,6},{3,7},{4,0},{5,1},{6,2},{7,3},{8,12},{9,13},{10,... | collective-permute-start | bytes 393224 | tf_op jit(solution)/shard_map/ppermute | solution.py:356
  4.7 8.6 %collective-permute-start = (bf16[64,1024]{1,0:T(8,128)(2,1)S(1)}, bf16[64,1024]{1,0:T(8,128)(2,1)S(1)}, u32[]{:S(2)}, u32[]{:S(2)}) collective-permute-start(bf16[64,1024]{1,0:T(8,128)(2,1)S(1)} %get-tuple-element.27.refs_2_), channel_id=1, source_target_pairs={{0,12},{1,13},{2,14},{3,15},{4,8},{5,9},{6,10},{7,11},{8,4},{9,5},... | collective-permute-start | bytes 393224 | tf_op jit(solution)/shard_map/ppermute | solution.py:356
  7.2 7.6 %collective-permute-start.10 = (bf16[64,1024]{1,0:T(8,128)(2,1)S(1)}, bf16[64,1024]{1,0:T(8,128)(2,1)S(1)}, u32[]{:S(2)}, u32[]{:S(2)}) collective-permute-start(bf16[64,1024]{1,0:T(8,128)(2,1)S(1)} %get-tuple-element.27.refs_2_), channel_id=1, source_target_pairs={{0,2},{1,3},{2,0},{3,1},{4,6},{5,7},{6,4},{7,5},{8,10},{9,11},{10,... | collective-permute-start | bytes 393224 | tf_op jit(solution)/shard_map/ppermute | solution.py:356
  8.7 6.9 %collective-permute-start.8 = (bf16[64,1024]{1,0:T(8,128)(2,1)S(1)}, bf16[64,1024]{1,0:T(8,128)(2,1)S(1)}, u32[]{:S(2)}, u32[]{:S(2)}) collective-permute-start(bf16[64,1024]{1,0:T(8,128)(2,1)S(1)} %collective-permute-done.7.refs_2_), channel_id=1, source_target_pairs={{0,2},{1,3},{2,0},{3,1},{4,6},{5,7},{6,4},{7,5},{8,10},{9,11},{10,... | collective-permute-start | bytes 393224 | tf_op jit(solution)/shard_map/ppermute | solution.py:356
  13.3 5.0 %collective-permute-start.5 = (bf16[64,1024]{1,0:T(8,128)(2,1)S(1)}, bf16[64,1024]{1,0:T(8,128)(2,1)S(1)}, u32[]{:S(2)}, u32[]{:S(2)}) collective-permute-start(bf16[64,1024]{1,0:T(8,128)(2,1)S(1)} %collective-permute-done.refs_2_), channel_id=1, source_target_pairs={{0,2},{1,3},{2,0},{3,1},{4,6},{5,7},{6,4},{7,5},{8,10},{9,11},{10,... | collective-permute-start | bytes 393224 | tf_op jit(solution)/shard_map/ppermute | solution.py:356
  14.9 12.7 %collective-permute-start.11 = (bf16[2,64,1024]{2,1,0:T(8,128)(2,1)S(1)}, bf16[2,64,1024]{2,1,0:T(8,128)(2,1)S(1)}, u32[]{:S(2)}, u32[]{:S(2)}) collective-permute-start(bf16[2,64,1024]{2,1,0:T(8,128)(2,1)S(1)} %pad_maximum_fusion.2), channel_id=1, source_target_pairs={{0,1},{1,0},{2,3},{3,2},{4,5},{5,4},{6,7},{7,6},{8,9},{9,8},{10,11... | collective-permute-start | bytes 786440 | tf_op jit(solution)/shard_map/ppermute | solution.py:356
  14.9 5.9 %collective-permute-start.1 = (bf16[64,1024]{1,0:T(8,128)(2,1)S(1)}, bf16[64,1024]{1,0:T(8,128)(2,1)S(1)}, u32[]{:S(2)}, u32[]{:S(2)}) collective-permute-start(bf16[64,1024]{1,0:T(8,128)(2,1)S(1)} %collective-permute-done.refs_2_), channel_id=1, source_target_pairs={{0,4},{1,5},{2,6},{3,7},{4,0},{5,1},{6,2},{7,3},{8,12},{9,13},{10,... | collective-permute-start | bytes 393224 | tf_op jit(solution)/shard_map/ppermute | solution.py:356
  15.6 12.8 %collective-permute-start.9 = (bf16[2,64,1024]{2,1,0:T(8,128)(2,1)S(1)}, bf16[2,64,1024]{2,1,0:T(8,128)(2,1)S(1)}, u32[]{:S(2)}, u32[]{:S(2)}) collective-permute-start(bf16[2,64,1024]{2,1,0:T(8,128)(2,1)S(1)} %pad_maximum_fusion.1), channel_id=1, source_target_pairs={{0,1},{1,0},{2,3},{3,2},{4,5},{5,4},{6,7},{7,6},{8,9},{9,8},{10,11... | collective-permute-start | bytes 786440 | tf_op jit(solution)/shard_map/ppermute | solution.py:356
  18.3 11.3 %collective-permute-start.6 = (bf16[2,64,1024]{2,1,0:T(8,128)(2,1)S(1)}, bf16[2,64,1024]{2,1,0:T(8,128)(2,1)S(1)}, u32[]{:S(2)}, u32[]{:S(2)}) collective-permute-start(bf16[2,64,1024]{2,1,0:T(8,128)(2,1)S(1)} %pad_maximum_fusion), channel_id=1, source_target_pairs={{0,1},{1,0},{2,3},{3,2},{4,5},{5,4},{6,7},{7,6},{8,9},{9,8},{10,11... | collective-permute-start | bytes 786440 | tf_op jit(solution)/shard_map/ppermute | solution.py:356
  20.8 5.0 %collective-permute-start.2 = (bf16[64,1024]{1,0:T(8,128)(2,1)S(1)}, bf16[64,1024]{1,0:T(8,128)(2,1)S(1)}, u32[]{:S(2)}, u32[]{:S(2)}) collective-permute-start(bf16[64,1024]{1,0:T(8,128)(2,1)S(1)} %collective-permute-done.1.refs_2_), channel_id=1, source_target_pairs={{0,2},{1,3},{2,0},{3,1},{4,6},{5,7},{6,4},{7,5},{8,10},{9,11},{10,... | collective-permute-start | bytes 393224 | tf_op jit(solution)/shard_map/ppermute | solution.py:356
  21.4 9.3 %collective-permute-start.4 = (bf16[64,1024]{1,0:T(8,128)(2,1)S(1)}, bf16[64,1024]{1,0:T(8,128)(2,1)S(1)}, u32[]{:S(2)}, u32[]{:S(2)}) collective-permute-start(bf16[64,1024]{1,0:T(8,128)(2,1)S(1)} %collective-permute-done.1.refs_2_), channel_id=1, source_target_pairs={{0,1},{1,0},{2,3},{3,2},{4,5},{5,4},{6,7},{7,6},{8,9},{9,8},{10,11... | collective-permute-start | bytes 393224 | tf_op jit(solution)/shard_map/ppermute | solution.py:356
  25.8 5.9 %collective-permute-start.3 = (bf16[1,64,1024]{2,1,0:T(8,128)(2,1)S(1)}, bf16[1,64,1024]{2,1,0:T(8,128)(2,1)S(1)}, u32[]{:S(2)}, u32[]{:S(2)}) collective-permute-start(bf16[1,64,1024]{2,1,0:T(8,128)(2,1)S(1)} %bitcast.14), channel_id=1, source_target_pairs={{0,1},{1,0},{2,3},{3,2},{4,5},{5,4},{6,7},{7,6},{8,9},{9,8},{10,11... | collective-permute-start | bytes 393224 | tf_op jit(solution)/shard_map/ppermute | solution.py:356
